TPU v7x, 32 devices: a whole 2x2x4 slice. The times are simulated.
32 devices in a mesh: site: 2 (over y), pts: 4 (over z), var: 2 (over x), cmp: 2 (over core).
Axes of the slice: x: 2, y: 2, z: 4, core: 2. Of those that a mesh axis runs over, the one named last changes fastest.
Arguments:
- sgt: bfloat16 [6, 3, 128, 4096], P('cmp', None, ('site', 'pts')), parts along dimension 2, may hold values from -6 to 6
- moment: float32 [6, 64], P('cmp', ('site', 'pts')), parts along dimension 1, may hold values from -6 to 6
- slip_spec: float32 [16, 2, 4096], replicated, may hold values from -3 to 3
- rp_slab: int32 [64], P('site'), parts along dimension 0, may hold values from 0 to 63, as said below
- rup_counts: int32 [8, 6], P(('site', 'pts')), parts along dimension 0, may hold values from 1 to 2, 8 in all within a row
- var_rupture: int32 [32], P('site'), parts along dimension 0, may hold values from 0 to 5
- var_source: int32 [32, 2], P('site'), parts along dimension 0, may hold values from 0 to 15
- owner_map: int32 [32], P('site'), parts along dimension 0, may hold values from 0 to 15, each once
Outputs:
- seismograms: float32 [32, 3, 4096], P(('site', 'pts', 'var', 'cmp')), parts along dimension 0
There are 2 independent parts, one for each index of `site`. A program takes and returns all parts, laid end to end along the dimension named above; an argument that names none is the same for every part. Nothing has to cross between parts.
Inputs may be any that keep to these rules, and one draw needn't show every extreme that they name: `rp_slab`: in each aligned block of 8 rupture-points (one owner's), at most 4 name slab points of one reader (slab points k * 16 to (k + 1) * 16 - 1 belong to reader k), and in every block some reader is named exactly 4 times. `rup_counts`: each row gives, for the ruptures in order, how many of that owner's 8 slots belong to each; every rupture has 1 or more on every owner, the row sums to 8, and some entry of each row is exactly 2. `owner_map`: A permutation of the variations.
All inputs are finite; a program needn't handle non-finite values.
Results may differ from a plain program's by a relative error of at most 0.0003.
Values may be sent and summed in bfloat16 or wider, within the bound.
A program may use at most 64 MiB of HBM per device.

v0:
```python
import math

import jax
import jax.numpy as jnp
from jax import lax
from jax.sharding import PartitionSpec as P

TAU = 4


highest = lax.Precision.HIGHEST


def cos_sin(numerator, period):
    angles = numerator.astype(jnp.float32) * (2.0 * math.pi / period)
    return (jnp.cos(angles), jnp.sin(angles))


def forward_spectra(signal):
    series, samples = signal.shape
    length = 2 * samples
    blocks = length // 128
    rows_half = blocks // 2
    row_iota = jnp.arange(rows_half, dtype=jnp.int32)
    outer_iota = jnp.arange(blocks, dtype=jnp.int32)
    lane_iota = jnp.arange(128, dtype=jnp.int32)
    half_iota = jnp.arange(64, dtype=jnp.int32)
    first_cos, first_sin = cos_sin(row_iota[:, None] * outer_iota[None, :] % blocks, blocks)
    first_table = jnp.concatenate([first_cos, -first_sin], axis=1)
    shaped = signal.reshape(series, rows_half, 128)
    first_pass = jnp.einsum("sab,am->smb", shaped, first_table, precision=highest)
    real_part = first_pass[:, :blocks]
    imag_part = first_pass[:, blocks:]
    turn_cos, turn_sin = cos_sin(outer_iota[:, None] * lane_iota[None, :], length)
    turned_real = real_part * turn_cos + imag_part * turn_sin
    turned_imag = imag_part * turn_cos - real_part * turn_sin
    second_cos, second_sin = cos_sin(lane_iota[:, None] * half_iota[None, :] % 128, 128)
    second_table = jnp.concatenate(
        [
            jnp.concatenate([second_cos, -second_sin], axis=1),
            jnp.concatenate([second_sin, second_cos], axis=1),
        ],
        axis=0,
    )
    joined = jnp.concatenate([turned_real, turned_imag], axis=-1)
    return jnp.einsum("skb,bm->skm", joined, second_table, precision=highest)


def inverse_series(spectra):
    series, blocks, lanes = spectra.shape
    samples = blocks * 64
    length = 2 * samples
    rows_half = blocks // 2
    outer_iota = jnp.arange(blocks, dtype=jnp.int32)
    lane_iota = jnp.arange(128, dtype=jnp.int32)
    half_iota = jnp.arange(64, dtype=jnp.int32)
    row_iota = jnp.arange(rows_half, dtype=jnp.int32)
    frequency = outer_iota[:, None] + blocks * half_iota[None, :]
    weights = jnp.where(frequency == 0, 1.0, 2.0).astype(jnp.float32) / length
    weights = jnp.concatenate([weights, weights], axis=-1)
    scaled = spectra * weights[None]
    third_cos, third_sin = cos_sin(half_iota[:, None] * lane_iota[None, :] % 128, 128)
    third_table = jnp.concatenate(
        [
            jnp.concatenate([third_cos, third_sin], axis=1),
            jnp.concatenate([-third_sin, third_cos], axis=1),
        ],
        axis=0,
    )
    middle = jnp.einsum("skm,mb->skb", scaled, third_table, precision=highest)
    mid_real = middle[..., :128]
    mid_imag = middle[..., 128:]
    turn_cos, turn_sin = cos_sin(outer_iota[:, None] * lane_iota[None, :], length)
    back_real = mid_real * turn_cos - mid_imag * turn_sin
    back_imag = mid_real * turn_sin + mid_imag * turn_cos
    stacked = jnp.concatenate([back_real, back_imag], axis=1)
    last_cos, last_sin = cos_sin(outer_iota[:, None] * row_iota[None, :] % blocks, blocks)
    last_table = jnp.concatenate([last_cos, -last_sin], axis=0)
    result = jnp.einsum("smb,ma->sab", stacked, last_table, precision=highest)
    return result.reshape(series, samples)


def per_device(sgt, moment, slip_spec, rp_slab, rup_counts, var_rupture, var_source, owner_map):
    comp_half, seis_comp, slab_dev, samples = sgt.shape
    rp_dev = moment.shape[1]
    owners = lax.axis_size("pts")
    my_owner = lax.axis_index("pts")
    var_count = lax.axis_size("var")
    my_var = lax.axis_index("var")
    cmp_count = lax.axis_size("cmp")
    my_core = lax.axis_index("cmp")
    capacity = max(2, (2 * rp_dev + owners - 1) // owners)
    length = 2 * samples
    blocks = length // 128
    readers = rp_slab // slab_dev
    within = rp_slab % slab_dev
    reader_rows = readers.reshape(owners, rp_dev)
    slot_iota = jnp.arange(rp_dev, dtype=jnp.int32)
    lower_slot = slot_iota[None, :] < slot_iota[:, None]
    same_reader = reader_rows[:, :, None] == reader_rows[:, None, :]
    ranks = jnp.sum(same_reader & lower_slot[None], axis=2)
    owner_ids = jnp.arange(owners, dtype=jnp.int32)[:, None]
    target = (owner_ids * capacity + ranks).reshape(-1)
    spill = owners * capacity
    place = jnp.where(readers == my_owner, target, spill)
    send_rows = jnp.zeros((spill,), jnp.int32).at[place].set(within, mode="drop")
    send_live = jnp.zeros((spill,), jnp.bool_).at[place].set(True, mode="drop")
    outgoing = jnp.take(sgt, send_rows, axis=2)
    outgoing = jnp.where(send_live[None, None, :, None], outgoing, jnp.zeros((), outgoing.dtype))
    received = lax.all_to_all(outgoing, "pts", split_axis=2, concat_axis=2, tiled=True)
    pick_rows = reader_rows[my_owner] * capacity + ranks[my_owner]
    picked = jnp.take(received, pick_rows, axis=2)
    partial_value = jnp.sum(moment[:, None, :, None] * picked.astype(jnp.float32), axis=0)
    pieces = lax.all_to_all(partial_value[None], "cmp", split_axis=2, concat_axis=0, tiled=True)
    half_sum = jnp.sum(pieces, axis=0)
    half_points = rp_dev // cmp_count
    half_spec = forward_spectra(half_sum.reshape(seis_comp * half_points, samples)).reshape(
        seis_comp, half_points, blocks, 128
    )
    spectra = lax.all_gather(half_spec, "cmp", axis=1, tiled=True)
    counts_all = lax.all_gather(rup_counts, "pts", axis=0, tiled=True)
    my_counts = rup_counts[0]
    ruptures = my_counts.shape[0]
    rupture_iota = jnp.arange(ruptures, dtype=jnp.int32)
    inclusive = jnp.cumsum(my_counts)
    rupture_of = jnp.sum(inclusive[None, :] <= slot_iota[:, None], axis=1)
    owner_mask = (jnp.arange(owners, dtype=jnp.int32) < my_owner)[:, None]
    before = jnp.sum(jnp.where(owner_mask, counts_all, 0), axis=0)
    lengths = jnp.sum(counts_all, axis=0)
    point_onehot = (rupture_of[:, None] == rupture_iota[None, :]).astype(jnp.int32)
    shift_table = before - inclusive + my_counts
    position = slot_iota + jnp.sum(point_onehot * shift_table[None, :], axis=1)
    outer_iota = jnp.arange(blocks, dtype=jnp.int32)
    half_iota = jnp.arange(64, dtype=jnp.int32)
    frequency = outer_iota[:, None] + blocks * half_iota[None, :]
    point_cos, point_sin = cos_sin(
        frequency[None] * (TAU * position)[:, None, None] % length, length
    )
    point_cos = point_cos[None]
    point_sin = point_sin[None]
    real_x = spectra[..., :64]
    imag_x = spectra[..., 64:]
    lagged = jnp.concatenate(
        [real_x * point_cos + imag_x * point_sin, imag_x * point_cos - real_x * point_sin], axis=-1
    )
    leading = jnp.concatenate(
        [real_x * point_cos - imag_x * point_sin, imag_x * point_cos + real_x * point_sin], axis=-1
    )
    per_owner = owner_map.shape[0] // (owners * var_count * cmp_count)
    row_owner = jnp.arange(owners, dtype=jnp.int32)[:, None]
    row_unit = jnp.arange(per_owner, dtype=jnp.int32)[None, :]
    slot_ids = (
        ((row_owner * var_count + my_var) * cmp_count + my_core) * per_owner + row_unit
    ).reshape(-1)
    var_ids = owner_map[slot_ids]
    var_rup = var_rupture[var_ids]
    hypo_index = var_source[var_ids, 0]
    slip_index = var_source[var_ids, 1]
    functions = slip_spec.shape[0]
    rup_onehot = (var_rup[:, None] == rupture_iota[None, :]).astype(jnp.int32)
    rup_length = jnp.sum(rup_onehot * lengths[None, :], axis=1)
    hypocenter = hypo_index * rup_length // functions
    same_rup = var_rup[:, None] == rupture_of[None, :]
    ahead_mask = (same_rup & (position[None, :] >= hypocenter[:, None])).astype(jnp.float32)
    behind_mask = (same_rup & (position[None, :] < hypocenter[:, None])).astype(jnp.float32)
    hypo_cos, hypo_sin = cos_sin(
        frequency[None] * (TAU * hypocenter)[:, None, None] % length, length
    )
    slip_rows = slip_spec[slip_index].reshape(slip_index.shape[0], 2, 64, blocks)
    slip_rows = jnp.transpose(slip_rows, (0, 3, 1, 2)).reshape(slip_index.shape[0], blocks, 128)
    first_sum = jnp.einsum("vq,cqkm->vckm", ahead_mask, lagged, precision=highest)
    second_sum = jnp.einsum("vq,cqkm->vckm", behind_mask, leading, precision=highest)
    rows_cos = hypo_cos[:, None]
    rows_sin = hypo_sin[:, None]
    rows_slip = slip_rows[:, None]
    sum_real = first_sum[..., :64] + second_sum[..., :64]
    diff_real = first_sum[..., :64] - second_sum[..., :64]
    sum_imag = first_sum[..., 64:] + second_sum[..., 64:]
    diff_imag = first_sum[..., 64:] - second_sum[..., 64:]
    turned_real = rows_cos * sum_real - rows_sin * diff_imag
    turned_imag = rows_cos * sum_imag + rows_sin * diff_real
    slip_real = rows_slip[..., :64]
    slip_imag = rows_slip[..., 64:]
    totals = lax.psum_scatter(
        jnp.concatenate(
            [
                slip_real * turned_real - slip_imag * turned_imag,
                slip_real * turned_imag + slip_imag * turned_real,
            ],
            axis=-1,
        ),
        "pts",
        scatter_dimension=0,
        tiled=True,
    )
    result = inverse_series(totals.reshape(per_owner * seis_comp, blocks, 128)).reshape(
        per_owner, seis_comp, samples
    )
    return result


def solution(mesh):
    placed = (
        P("cmp", None, ("site", "pts"), None),
        P("cmp", ("site", "pts")),
        P(),
        P("site"),
        P(("site", "pts"), None),
        P("site"),
        P("site", None),
        P("site"),
    )
    return jax.shard_map(
        per_device,
        mesh=mesh,
        in_specs=placed,
        out_specs=P(("site", "pts", "var", "cmp"), None, None),
        check_vma=False,
    )
```

profile of v0, /device:TPU:0, one launch (start us, length us, event | category | flops | bytes accessed | tf_op | source)
XLA Modules:
  0.0 121.4 jit_solution(11977667582550914608)
XLA Ops:
  6.6 0.8 and_select_fusion
  7.8 0.7 scatter_custom_fusion.1
  8.5 3.9 %gather_fusion.5 = bf16[16,3,3,4096]{3,0,2,1:T(8,128)(2,1)S(1)} fusion(bf16[3,3,16,4096]{3,2,1,0:T(8,128)(2,1)S(1)} %copy-done, s32[1024]{0:T(1024)S(1)} %pad_clamp_fusion.1), kind=kCustom, calls=%fused_computation.5 | custom fusion | bytes 2359360 | tf_op jit(solution)/shard_map/jit(_take)/gather | solution.py:108
  12.5 0.7 scatter_custom_fusion
  13.3 2.2 %copy.52 = bf16[3,3,16,4096]{3,1,0,2:T(4,128)(2,1)} copy(bf16[3,3,16,4096]{3,2,1,0:T(8,128)(2,1)S(1)} %select_bitcast_fusion) | data formatting | bytes 2359296 | tf_op jit(solution)/shard_map/jit(_where)/select_n | solution.py:109
  15.5 6.5 %all-to-all-start = ((bf16[3,3,16,4096]{3,1,0,2:T(4,128)(2,1)}), bf16[3,3,16,4096]{3,1,0,2:T(4,128)(2,1)S(1)}, u32[]{:S(2)}, u32[]{:S(2)}) async-start(bf16[3,3,16,4096]{3,1,0,2:T(4,128)(2,1)} %copy.52), calls=%async_computation | async-start | bytes 3145728 | tf_op jit(solution)/shard_map/all_to_all | solution.py:110
  22.0 0.7 sine_negate_fusion
  23.4 30.0 %all-gather = s32[4,1,6]{2,1,0:T(1,128)S(1)} all-gather(s32[1,1,6]{2,1,0:T(1,128)S(1)} %bitcast.102), channel_id=1, replica_groups=mesh['site'=2,'pts'=4,'var'=2,'cmp'=2] {'pts'}, dimensions={0}, use_global_device_ids=true | all-gather | bytes 120 | tf_op jit(solution)/shard_map/all_gather | solution.py:121
  53.8 0.6 gather_fusion
  54.5 0.6 gather_fusion.3
  55.2 0.6 gather_fusion.1
  55.8 1.7 %gather_fusion.2 = f32[4,2,4096]{2,1,0:T(2,128)S(1)} fusion(f32[16,2,4096]{2,1,0:T(2,128)} %param.10, s32[1024]{0:T(1024)S(1)} %pad_clamp_fusion.3), kind=kCustom, calls=%fused_computation.2 | custom fusion | bytes 262160 | tf_op jit(solution)/shard_map/gather | solution.py:169
  58.0 0.6 gather_fusion.4
  59.0 0.8 fusion.56
  59.8 0.9 fusion.61
  60.7 0.9 fusion.54
  62.2 1.9 %fusion.48 = (f32[4,64,64]{2,0,1:T(4,128)}, f32[4,64,64]{2,0,1:T(4,128)}) fusion(s32[4]{0:T(128)S(1)} %get-tuple-element.8, s32[64,64]{1,0:T(8,128)S(1)} %iota_add_fusion), kind=kLoop, calls=%fused_computation.89 | loop fusion | flops 229376 | bytes 147472 | tf_op jit(solution)/shard_map/cos | solution.py:16
  64.0 1.1 fusion.41
  65.1 1.8 %copy.53 = bf16[3,3,16,4096]{3,1,2,0:T(4,128)(2,1)} copy(bf16[3,3,16,4096]{3,1,0,2:T(4,128)(2,1)S(1)} %all-to-all-done) | data formatting | bytes 2359296 | tf_op jit(solution)/shard_map/all_to_all | solution.py:110
  67.0 2.6 %gather_fusion.6 = bf16[8,3,3,4096]{3,2,1,0:T(4,128)(2,1)S(1)} fusion(bf16[3,3,16,4096]{3,1,2,0:T(4,128)(2,1)} %copy.53, s32[1024]{0:T(1024)S(1)} %pad_clamp_fusion), kind=kCustom, calls=%fused_computation.6 | custom fusion | bytes 1179680 | tf_op jit(solution)/shard_map/jit(_take)/gather | solution.py:112
  69.6 0.7 fusion
  70.7 4.0 %all_to_all.17 = f32[1,3,8,4096]{3,0,1,2:T(1,128)S(1)} all-to-all(f32[1,3,8,4096]{3,0,1,2:T(1,128)S(1)} %copy.54), channel_id=1, replica_groups=mesh['site'=2,'pts'=4,'var'=2,'cmp'=2] {'cmp'}, dimensions={2} | all-to-all | bytes 786432 | tf_op jit(solution)/shard_map/all_to_all | solution.py:114
  75.6 0.9 convolution_bitcast_fusion
  76.7 0.9 fusion.1
  77.6 2.4 %all_gather.7 = f32[3,8,64,128]{3,2,0,1:T(8,128)S(1)} all-gather(f32[3,4,64,128]{3,2,0,1:T(8,128)S(1)} %copy.58), channel_id=1, replica_groups=mesh['site'=2,'pts'=4,'var'=2,'cmp'=2] {'cmp'}, dimensions={1}, use_global_device_ids=true | all-gather | bytes 1179648 | tf_op jit(solution)/shard_map/all_gather | solution.py:120
  80.3 1.0 fusion.14
  81.3 0.6 fusion.5
  81.9 0.6 fusion.9
  83.8 0.8 copy.61
  85.0 27.4 %reduce-scatter.2.cloned.1.call-done = f32[1,3,64,128]{3,2,1,0:T(8,128)} async-done(((f32[4,3,64,128]{3,2,1,0:T(8,128)}), f32[1,3,64,128]{3,2,1,0:T(8,128)}) %reduce-scatter.2.cloned.1.call-update) | async-done | bytes 98320 | tf_op jit(solution)/shard_map/reduce_scatter | solution.py:184
  112.4 1.2 fusion.33
  113.6 0.9 fusion.20
  (99 shorter events, 6.4 us)
Async XLA Ops:
  6.5 2.0 %copy-start = (bf16[3,3,16,4096]{3,2,1,0:T(8,128)(2,1)S(1)}, bf16[3,3,16,4096]{3,2,1,0:T(8,128)(2,1)}, u32[]{:S(2)}) copy-start(bf16[3,3,16,4096]{3,2,1,0:T(8,128)(2,1)} %param.8) | copy-start | bytes 3538948
  15.5 7.8 %copy-start.19 = (f32[3,8]{1,0:T(4,128)S(1)}, f32[3,8]{1,0:T(4,128)}, u32[]{:S(2)}) copy-start(f32[3,8]{1,0:T(4,128)} %param.9) | copy-start | bytes 292
  15.5 7.9 %copy-start.20 = (s32[1,6]{1,0:T(1,128)S(1)}, s32[1,6]{1,0:T(1,128)}, u32[]{:S(2)}) copy-start(s32[1,6]{1,0:T(1,128)} %param.12) | copy-start | bytes 76
  15.5 38.3 %copy-start.2 = (s32[16]{0:T(128)S(1)}, s32[16]{0:T(128)}, u32[]{:S(2)}) copy-start(s32[16]{0:T(128)} %param.15) | copy-start | bytes 196
  15.5 39.0 %copy-start.1 = (s32[16,2]{0,1:T(2,128)S(1)}, s32[16,2]{0,1:T(2,128)}, u32[]{:S(2)}) copy-start(s32[16,2]{0,1:T(2,128)} %param.14) | copy-start | bytes 388
  15.5 49.6 %all-to-all-start = ((bf16[3,3,16,4096]{3,1,0,2:T(4,128)(2,1)}), bf16[3,3,16,4096]{3,1,0,2:T(4,128)(2,1)S(1)}, u32[]{:S(2)}, u32[]{:S(2)}) async-start(bf16[3,3,16,4096]{3,1,0,2:T(4,128)(2,1)} %copy.52), calls=%async_computation | async-start | bytes 3145728 | tf_op jit(solution)/shard_map/all_to_all | solution.py:110
  22.0 90.4 %reduce-scatter.2.cloned.1.call-start = ((), (), s32[]{:S(2)}) async-start(), calls=%async_computation.3 | async-start | bytes 491520 | tf_op jit(solution)/shard_map/reduce_scatter | solution.py:184
  53.8 4.9 %copy-start.13 = (s32[8]{0:T(128)}, s32[8]{0:T(128)S(1)}, u32[]{:S(2)}) copy-start(s32[8]{0:T(128)S(1)} %convert_reduce_fusion.1) | copy-start | bytes 100
  55.2 2.9 %copy-start.3 = (s32[16]{0:T(128)S(1)}, s32[16]{0:T(128)}, u32[]{:S(2)}) copy-start(s32[16]{0:T(128)} %param.13) | copy-start | bytes 196
  58.7 5.4 %copy-start.15 = (s32[64]{0:T(128)}, s32[64]{0:T(128)S(1)}, u32[]{:S(2)}) copy-start(s32[64]{0:T(128)S(1)} %iota_multiply_fusion.2) | copy-start | bytes 772
  67.0 2.6 %copy-start.18 = (pred[8]{0:T(512)(128)(4,1)S(1)}, pred[8]{0:T(512)(128)(4,1)}, u32[]{:S(2)}) copy-start(pred[8]{0:T(512)(128)(4,1)} %get-tuple-element.10) | copy-start | bytes 28
  74.8 0.8 copy-start.11
  74.8 0.8 copy-start.12
  75.1 1.4 %copy-start.6 = (f32[64,128]{1,0:T(8,128)S(1)}, f32[64,128]{1,0:T(8,128)}, u32[]{:S(2)}) copy-start(f32[64,128]{1,0:T(8,128)} %get-tuple-element.37) | copy-start | bytes 98308
  75.1 1.4 %copy-start.7 = (f32[64,128]{1,0:T(8,128)S(1)}, f32[64,128]{1,0:T(8,128)}, u32[]{:S(2)}) copy-start(f32[64,128]{1,0:T(8,128)} %get-tuple-element.38) | copy-start | bytes 98308
  75.6 1.1 copy-start.8
  75.6 1.1 copy-start.9
  75.6 1.1 copy-start.10
  80.2 1.0 copy-start.14
  80.2 1.0 copy-start.17
  81.9 0.9 copy-start.4
  81.9 1.0 copy-start.5
  83.5 1.3 %copy-start.16 = (s32[64]{0:T(128)S(1)}, s32[64]{0:T(128)}, u32[]{:S(2)}) copy-start(s32[64]{0:T(128)} %copy-done.15) | copy-start | bytes 772
Sparse Core Ops, SparseCore 0:
  84.7 27.6 reduce-scatter.1
where the time goes:
time: 122 us; the launch traced here: 121 us
  blocking collectives  36.4 us (30%)
  waiting for transfers between devices  27.4 us (22%)
  local copies, waits for them, and re-layouts  19.3 us (16%)
  between operations  13.9 us (11%)
  other arithmetic  12.7 us (10%)
  starting transfers between devices  6.49 us (5%)
  matrix products  5.1 us (4%)
    all_gather x1, blocking collectives, per_device(): counts_all = lax.all_gather(rup_counts, 'pts', axis=0, tiled=True)  30 us
    reduce_scatter x1, waiting for transfers between devices, per_device(): lax.psum_scatter(jnp.concatenate([slip_real * turned_real - slip_imag * t...  27.4 us
    all_to_all x1, starting transfers between devices, per_device(): lax.all_to_all(outgoing, 'pts', split_axis=2, concat_axis=2, tiled=True)  6.49 us
    all_to_all x1, blocking collectives, per_device(): lax.all_to_all(partial_value[None], 'cmp', split_axis=2, concat_axis=0, t...  4.05 us
    gather x1, local copies, waits for them, and re-layouts, per_device(): outgoing = jnp.take(sgt, send_rows, axis=2)  3.92 us
    cos x3, other arithmetic, cos_sin(): return (jnp.cos(angles), jnp.sin(angles))  3.1 us
    gather x1, local copies, waits for them, and re-layouts, per_device(): picked = jnp.take(received, pick_rows, axis=2)  2.62 us
  transfers between devices with their start and end apart: 2, of which 1 were waited for; matrix products, arithmetic and copies ran while one was open for 11% of the time, Pallas kernels for 0%

commit v1 on v0

v1 whole, which is shorter than its diff:
```python
import functools
import math

import jax
import jax.numpy as jnp
import numpy as np
from jax import lax
from jax.experimental import pallas as pl
from jax.experimental.pallas import tpu as pltpu
from jax.sharding import PartitionSpec as P

TAU = 4
MOST = 2
LANES = 128
MESH = pl.DeviceIdType.MESH
HIGHEST = lax.Precision.HIGHEST


def ceil_to(value, unit):
    return (value + unit - 1) // unit * unit


def tables(comps, samples, tail_rows, row_pitch):
    length = 2 * samples
    blocks = length // LANES
    half = blocks // 2
    outer = np.arange(blocks)

    def angle(numer, period):
        return 2.0 * np.pi * (numer % period) / period

    first = np.zeros((comps, 2 * blocks, row_pitch))
    for c in range(comps):
        for t1 in range(half + tail_rows):
            row = c * half + t1 if t1 < half else comps * half + (t1 - half) * comps + c
            turn = angle(outer * t1, blocks)
            first[c, :blocks, row] = np.cos(turn)
            first[c, blocks:, row] = -np.sin(turn)
    first = first.reshape(comps * 2 * blocks, row_pitch)
    lane = np.arange(LANES)
    turn = angle(outer[:, None] * lane[None, :], length)
    twiddle = np.stack([np.cos(turn), np.sin(turn)])
    group = lane // half
    k2 = 2 * (lane % half) + group // 2
    imag = group % 2
    turn = angle(lane[:, None] * k2[None, :], LANES)
    cos, sin = np.cos(turn), np.sin(turn)
    top = np.where(imag[None] == 1, -sin, cos)
    bottom = np.where(imag[None] == 1, cos, sin)
    top_swap = np.where(imag[None] == 0, -sin, cos)
    bottom_swap = np.where(imag[None] == 0, cos, sin)
    second = np.concatenate(
        [np.concatenate([top, top_swap], 1), np.concatenate([bottom, bottom_swap], 1)], 0
    )
    turn = angle(k2[:, None] * lane[None, :], LANES)
    cos, sin = np.cos(turn), np.sin(turn)
    third = np.concatenate(
        [np.where(imag[:, None] == 1, -sin, cos), np.where(imag[:, None] == 1, cos, sin)], 1
    )
    turn = angle(np.arange(half)[:, None] * outer[None, :], blocks)
    last = np.concatenate([np.cos(turn), -np.sin(turn)], 1)
    weight = np.full((blocks, LANES), 2.0 / length)
    weight[0, (lane % half == 0) & (group // 2 == 0)] = 1.0 / length
    return [np.asarray(t, np.float32) for t in (first, twiddle, second, third, last, weight)]


def dot(a, b, contract=(1, 0)):
    return lax.dot_general(
        a,
        b,
        (((contract[0],), (contract[1],)), ((), ())),
        precision=HIGHEST,
        preferred_element_type=jnp.float32,
    )


def kernel(
    dims,
    counts_ref,
    moment_ref,
    rupture_ref,
    source_ref,
    owner_ref,
    slab_ref,
    sgt_hbm,
    slip_hbm,
    first_hbm,
    twiddle_hbm,
    second_hbm,
    third_hbm,
    last_hbm,
    weight_hbm,
    out_ref,
    sgt_ref,
    slip_ref,
    first_ref,
    twiddle_ref,
    second_ref,
    third_ref,
    last_ref,
    weight_ref,
    meta_ref,
    slabs_ref,
    spect_ref,
    acc_ref,
    mine_ref,
    pair_ref,
    sums_ref,
    ring_ref,
    load_sem,
    meta_send,
    meta_recv,
    pair_send,
    pair_recv,
    ring_send,
    ring_recv,
):
    owners, variants, cores, lanes_q, delays, pitch, tail_rows = dims
    moments, comps, slab_dev, samples = sgt_ref.shape
    ruptures = counts_ref.shape[1]
    rp_dev = moment_ref.shape[1]
    nrp = slab_ref.shape[1]
    functions = slip_ref.shape[0]
    half = samples // LANES
    blocks = 2 * half
    nv = owners * cores
    me = lax.axis_index("pts")
    my_var = lax.axis_index("var")
    my_core = lax.axis_index("cmp")

    barrier = pltpu.get_barrier_semaphore()
    for d in range(1, owners):
        pl.semaphore_signal(
            barrier, inc=1, device_id={"pts": lax.rem(me + d, owners)}, device_id_type=MESH
        )
    for c in range(1, cores):
        pl.semaphore_signal(
            barrier, inc=1, device_id={"cmp": lax.rem(my_core + c, cores)}, device_id_type=MESH
        )
    loads = []
    for i, (src, dst) in enumerate(
        (
            (slip_hbm, slip_ref),
            (sgt_hbm, sgt_ref),
            (weight_hbm, weight_ref),
            (first_hbm, first_ref),
            (twiddle_hbm, twiddle_ref),
            (second_hbm, second_ref),
            (third_hbm, third_ref),
            (last_hbm, last_ref),
        )
    ):
        copy = pltpu.make_async_copy(src, dst, load_sem.at[i])
        copy.start()
        loads.append(copy)

    lane = lax.broadcasted_iota(jnp.int32, (1, lanes_q), 1)
    start = me * rp_dev
    slot = lane - start
    inside = (slot >= 0) & (slot < rp_dev)
    zero = jnp.zeros((1, lanes_q), jnp.float32)
    meta_ref[0] = jnp.zeros(meta_ref.shape[1:], jnp.float32)
    for j in range(moments):
        row = zero
        for l in range(rp_dev):
            row = jnp.where(slot == l, moment_ref[j, l], row)
        meta_ref[0, j : j + 1, :] = row
    total = jnp.int32(0)
    rup_row = jnp.zeros((1, lanes_q), jnp.int32)
    begin_row = jnp.zeros((1, lanes_q), jnp.int32)
    for r in range(ruptures):
        count = counts_ref[0, r]
        total = total + count
        passed = total <= slot
        rup_row = rup_row + passed.astype(jnp.int32)
        begin_row = jnp.where(passed, total, begin_row)
        value = count.astype(jnp.float32)
        meta_ref[0, 8 + r : 9 + r, :] = jnp.where(lane >= start + rp_dev, value, 0.0)
        meta_ref[0, 16 + r : 17 + r, :] = zero + value
    meta_ref[0, moments : moments + 1, :] = jnp.where(inside, rup_row.astype(jnp.float32), 0.0)
    meta_ref[0, moments + 1 : moments + 2, :] = jnp.where(
        inside, (slot - begin_row).astype(jnp.float32), 0.0
    )
    slabs_ref[...] = jnp.full(slabs_ref.shape, -1, jnp.int32)
    slabs_ref[:, :nrp] = slab_ref[...]

    rup_v = jnp.zeros((nv, lanes_q), jnp.float32)
    src_v = jnp.zeros((nv, lanes_q), jnp.float32)
    v_iota = lax.broadcasted_iota(jnp.int32, (nv, lanes_q), 0)
    my_slip = jnp.int32(0)
    for i in range(nv):
        p = lax.rem(me + i % owners, owners)
        c = lax.rem(my_core + i // owners, cores)
        var_id = owner_ref[(p * variants + my_var) * cores + c]
        rup_v = jnp.where(v_iota == i, rupture_ref[var_id].astype(jnp.float32), rup_v)
        src_v = jnp.where(v_iota == i, source_ref[var_id, 0].astype(jnp.float32), src_v)
        if i == 0:
            my_slip = source_ref[var_id, 1]

    pl.semaphore_wait(barrier, owners + cores - 2)
    metas = []
    for d in range(1, owners):
        copy = pltpu.make_async_remote_copy(
            src_ref=meta_ref.at[0],
            dst_ref=meta_ref.at[d],
            send_sem=meta_send.at[d],
            recv_sem=meta_recv.at[d],
            device_id={"pts": lax.rem(me + d, owners)},
            device_id_type=MESH,
        )
        copy.start()
        metas.append(copy)

    loads[0].wait()
    for a in range(half):
        real = slip_ref[my_slip, 0:1, a * LANES : (a + 1) * LANES]
        imag = slip_ref[my_slip, 1:2, a * LANES : (a + 1) * LANES]
        spect_ref[a : a + 1, :] = real
        spect_ref[half + a : half + a + 1, :] = real
        spect_ref[2 * half + a : 2 * half + a + 1, :] = -imag
        spect_ref[3 * half + a : 3 * half + a + 1, :] = imag
    turned = jnp.transpose(spect_ref[...])
    loads[2].wait()
    slip_real = weight_ref[...] * jnp.concatenate(
        [turned[:blocks, :blocks], turned[blocks:, :blocks]], axis=1
    )
    slip_imag = weight_ref[...] * jnp.concatenate(
        [turned[:blocks, blocks:], turned[blocks:, blocks:]], axis=1
    )
    spect_ref[:blocks, :] = slip_real
    spect_ref[blocks:, :] = slip_imag

    loads[1].wait()
    for copy in metas:
        copy.wait()
    merged = meta_ref[0]
    for d in range(1, owners):
        merged = merged + meta_ref[d]
    rup_row = merged[moments : moments + 1]
    pos_row = merged[moments + 1 : moments + 2]
    len_v = jnp.zeros((nv, lanes_q), jnp.float32)
    for r in range(ruptures):
        pos_row = pos_row + jnp.where(rup_row == r, merged[8 + r : 9 + r], 0.0)
        len_v = len_v + jnp.where(rup_v == r, merged[16 + r : 17 + r], 0.0)
    hyp_v = jnp.floor((src_v * len_v + 0.5) * (1.0 / functions))
    apart = jnp.where(rup_v == rup_row, jnp.abs(pos_row - hyp_v), -1.0)
    local = slabs_ref[...] - me * slab_dev
    s_iota = lax.broadcasted_iota(jnp.int32, (slab_dev, lanes_q), 0)
    hit = s_iota == local
    spread = jnp.concatenate(
        [jnp.where(hit, merged[j : j + 1], 0.0) for j in range(moments)] * 2, axis=0
    )
    depth = moments * slab_dev
    upper = lax.broadcasted_iota(jnp.int32, (1, 2 * depth), 1) < depth
    group = delays
    while group * nv > 64 and group % 2 == 0:
        group //= 2
    groups = delays // group
    width = samples + tail_rows * LANES
    if groups > 1:
        acc_ref[...] = jnp.zeros(acc_ref.shape, jnp.float32)

    def one_group(step, carry):
        base = (groups - 1 - step) * group
        picks = jnp.concatenate(
            [
                (apart == jnp.float32(delta) + lax.convert_element_type(base, jnp.float32)).astype(
                    jnp.float32
                )
                for delta in range(group)
            ],
            axis=0,
        )
        weights = dot(picks, spread, (1, 1))
        coarse = weights.astype(jnp.bfloat16)
        fine = (weights - coarse.astype(jnp.float32)).astype(jnp.bfloat16)
        pieces = jnp.where(upper, coarse.astype(jnp.float32), fine.astype(jnp.float32)).astype(
            jnp.bfloat16
        )
        pad = jnp.zeros((nv, width - samples), jnp.float32)
        for c in range(comps):
            series = jnp.concatenate([sgt_ref[j, c] for j in range(moments)] * 2, axis=0)
            product = jnp.dot(pieces, series, preferred_element_type=jnp.float32)
            acc = acc_ref[c] if groups > 1 else None
            for delta in reversed(range(group)):
                term = jnp.concatenate([product[delta * nv : (delta + 1) * nv], pad], axis=1)
                acc = term if acc is None else pltpu.roll(acc, TAU, 1) + term
            if groups > 1:
                acc_ref[c] = acc
            else:
                emit(c, acc)
        return carry

    def emit(c, acc):
        for t1 in range(half + tail_rows):
            row = c * half + t1 if t1 < half else comps * half + (t1 - half) * comps + c
            for b in range(nv // 8):
                mine_ref[pl.ds(b * 8 * pitch + row, 8, stride=pitch), :] = acc[
                    b * 8 : (b + 1) * 8, t1 * LANES : (t1 + 1) * LANES
                ]

    used = comps * (half + tail_rows)
    for i in range(nv):
        if used < pitch:
            mine_ref[i * pitch + used : (i + 1) * pitch, :] = jnp.zeros(
                (pitch - used, LANES), jnp.float32
            )
    if groups > 1:
        lax.fori_loop(0, groups, one_group, 0)
        for c in range(comps):
            emit(c, acc_ref[c])
    else:
        one_group(0, 0)

    size = owners * pitch
    pairs = []
    for c in range(1, cores):
        copy = pltpu.make_async_remote_copy(
            src_ref=mine_ref.at[pl.ds(c * size, size)],
            dst_ref=pair_ref.at[c - 1],
            send_sem=pair_send.at[c - 1],
            recv_sem=pair_recv.at[c - 1],
            device_id={"cmp": lax.rem(my_core + c, cores)},
            device_id_type=MESH,
        )
        copy.start()
        pairs.append(copy)
    for copy in loads[3:]:
        copy.wait()
    for copy in pairs:
        copy.wait_recv()
    order = sorted(range(1, owners), key=lambda d: -min(d, owners - d))

    def joined(d):
        value = mine_ref[d * pitch : (d + 1) * pitch, :]
        for c in range(1, cores):
            value = value + pair_ref[c - 1, d * pitch : (d + 1) * pitch, :]
        return value

    for d in order:
        sums_ref[d - 1] = joined(d)
    rings = []
    for d in order:
        copy = pltpu.make_async_remote_copy(
            src_ref=sums_ref.at[d - 1],
            dst_ref=ring_ref.at[d - 1],
            send_sem=ring_send.at[d - 1],
            recv_sem=ring_recv.at[d - 1],
            device_id={"pts": lax.rem(me + d, owners)},
            device_id_type=MESH,
        )
        copy.start()
        rings.append(copy)
    packed = joined(0)
    for copy in rings:
        copy.wait_recv()
    for d in range(1, owners):
        packed = packed + ring_ref[d - 1]

    stage = dot(first_ref[...], packed)
    cos, sin = twiddle_ref[0], twiddle_ref[1]
    rows = []
    for c in range(comps):
        real = stage[2 * c * blocks : (2 * c + 1) * blocks]
        imag = stage[(2 * c + 1) * blocks : (2 * c + 2) * blocks]
        rows.append(
            jnp.concatenate([real * cos + imag * sin, imag * cos - real * sin], axis=1)
        )
    spectra = dot(jnp.concatenate(rows, axis=0), second_ref[...])
    slip_real, slip_imag = spect_ref[:blocks, :], spect_ref[blocks:, :]
    rows = []
    for c in range(comps):
        part = spectra[c * blocks : (c + 1) * blocks]
        rows.append(part[:, :LANES] * slip_real + part[:, LANES:] * slip_imag)
    middle = dot(jnp.concatenate(rows, axis=0), third_ref[...])
    columns = []
    for c in range(comps):
        real = middle[c * blocks : (c + 1) * blocks, :LANES]
        imag = middle[c * blocks : (c + 1) * blocks, LANES:]
        columns.append(
            jnp.concatenate([real * cos - imag * sin, real * sin + imag * cos], axis=0)
        )
    result = dot(last_ref[...], jnp.concatenate(columns, axis=1))
    for c in range(comps):
        out_ref[c] = result[:, c * LANES : (c + 1) * LANES]
    for copy in pairs + rings:
        copy.wait_send()


def per_device(owners, variants, cores, *args):
    sgt, moment, slip_spec, rp_slab, rup_counts, var_rupture, var_source, owner_map = args
    moments, comps, slab_dev, samples = sgt.shape
    nrp = rp_slab.shape[0]
    half = samples // LANES
    nv = owners * cores
    assert owner_map.shape[0] == nv * variants and 4 * half == LANES and nv % 8 == 0
    assert moments + 2 <= 8 and rup_counts.shape[1] <= 8
    lanes_q = ceil_to(nrp, LANES)
    delays = MOST * owners
    tail_rows = ceil_to(TAU * (delays - 1), LANES) // LANES
    width = samples + tail_rows * LANES
    pitch = ceil_to(comps * (half + tail_rows), 8)
    consts = tables(comps, samples, tail_rows, pitch)
    dims = (owners, variants, cores, lanes_q, delays, pitch, tail_rows)
    f32 = jnp.float32
    others = max(owners - 1, 1)
    smem = pl.BlockSpec(memory_space=pltpu.SMEM)
    vmem = pl.BlockSpec(memory_space=pltpu.VMEM)
    anywhere = pl.BlockSpec(memory_space=pl.ANY)
    out = pl.pallas_call(
        functools.partial(kernel, dims),
        out_shape=jax.ShapeDtypeStruct((comps, half, LANES), f32),
        in_specs=[smem] * 5 + [vmem] + [anywhere] * 8,
        out_specs=vmem,
        scratch_shapes=[
            pltpu.VMEM(sgt.shape, sgt.dtype),
            pltpu.VMEM(slip_spec.shape, f32),
            *[pltpu.VMEM(t.shape, f32) for t in consts],
            pltpu.VMEM((owners, 24, lanes_q), f32),
            pltpu.VMEM((1, lanes_q), jnp.int32),
            pltpu.VMEM((LANES, LANES), f32),
            pltpu.VMEM((comps, nv, width) if nv * delays > 64 else (1, 8, LANES), f32),
            pltpu.VMEM((nv * pitch, LANES), f32),
            pltpu.VMEM((cores - 1, owners * pitch, LANES), f32),
            pltpu.VMEM((others, pitch, LANES), f32),
            pltpu.VMEM((others, pitch, LANES), f32),
            pltpu.SemaphoreType.DMA((8,)),
            pltpu.SemaphoreType.DMA((owners,)),
            pltpu.SemaphoreType.DMA((owners,)),
            pltpu.SemaphoreType.DMA((cores,)),
            pltpu.SemaphoreType.DMA((cores,)),
            pltpu.SemaphoreType.DMA((owners,)),
            pltpu.SemaphoreType.DMA((owners,)),
        ],
        compiler_params=pltpu.CompilerParams(collective_id=0, has_side_effects=True),
    )(
        rup_counts,
        moment,
        var_rupture,
        var_source,
        owner_map,
        rp_slab.reshape(1, nrp),
        sgt,
        slip_spec,
        *[jnp.asarray(t) for t in consts],
    )
    return out.reshape(1, comps, samples)


def solution(mesh):
    placed = (
        P("cmp", None, ("site", "pts"), None),
        P("cmp", ("site", "pts")),
        P(),
        P("site"),
        P(("site", "pts"), None),
        P("site"),
        P("site", None),
        P("site"),
    )
    sizes = (mesh.shape["pts"], mesh.shape["var"], mesh.shape["cmp"])
    return jax.shard_map(
        functools.partial(per_device, *sizes),
        mesh=mesh,
        in_specs=placed,
        out_specs=P(("site", "pts", "var", "cmp"), None, None),
        check_vma=False,
    )
```

time: 122 us -> 22.4 us (0.18)
  the two profiles are of different devices: /device:TPU:0 before, /device:TPU:1 now
where the time goes in v1:
time: 22.4 us; the launch traced here: 22.2 us
  Pallas kernels  19.4 us (87%)
  local copies, waits for them, and re-layouts  2.77 us (12%)
    pallas_call x1, Pallas kernels, per_device(): pl.pallas_call(functools.partial(kernel, dims), out_shape=jax.ShapeDtypeS...  19.4 us
    unnamed x2, local copies, waits for them, and re-layouts  2.77 us

profile of v1, /device:TPU:1, one launch (start us, length us, event | category | flops | bytes accessed | tf_op | source)
XLA Modules:
  0.0 22.2 jit_solution(18241754281197584859)
XLA Ops:
  0.0 1.4 %copy.17.source_ref = s32[16,2]{1,0:T(8,128)} copy(s32[16,2]{0,1:T(2,128)} %param.20) | data formatting | bytes 256 | tf_op args[6]
  1.4 19.4 %shard_map.136 = f32[3,32,128]{2,1,0:T(8,128)} custom-call(s32[1,6]{1,0:T(1,128)} %counts_ref.1, f32[3,8]{1,0:T(4,128)} %moment_ref.1, s32[16]{0:T(128)} %rupture_ref.1, s32[16,2]{1,0:T(8,128)} %copy.17.source_ref, s32[16]{0:T(128)} %owner_ref.1, s32[1,32]{1,0:T(1,128)} %bitcast.3, bf16[3,3,16,4096]{3,2,1,0:T(8,128)(2,1)} %sgt_hbm.1, ...), custom_call_target="tpu_custom_call" | custom-call | tf_op jit(solution)/shard_map/pallas_call | solution.py:410
  20.7 1.4 %copy.20 = f32[1,3,4096]{2,0,1:T(1,128)} copy(f32[1,3,4096]{2,0,1:T(1,128)} %bitcast.2) | data formatting | bytes 98304

commit v2 on v1

v2 whole, which is shorter than its diff:
```python
import functools
import math

import jax
import jax.numpy as jnp
import numpy as np
from jax import lax
from jax.experimental import pallas as pl
from jax.experimental.pallas import tpu as pltpu
from jax.sharding import PartitionSpec as P

TAU = 4
MOST = 2
LANES = 128
MESH = pl.DeviceIdType.MESH
HIGHEST = lax.Precision.HIGHEST


def ceil_to(value, unit):
    return (value + unit - 1) // unit * unit


def tables(comps, samples, tail_rows, tail_block):
    length = 2 * samples
    blocks = length // LANES
    half = blocks // 2
    outer = np.arange(blocks)

    def angle(numer, period):
        return 2.0 * np.pi * (numer % period) / period

    first = np.zeros((comps, 2 * blocks, tail_block + half))
    for c in range(comps):
        for t1 in range(half + tail_rows):
            row = tail_block + t1 if t1 < half else (t1 - half) * comps + c
            turn = angle(outer * t1, blocks)
            first[c, :blocks, row] = np.cos(turn)
            first[c, blocks:, row] = -np.sin(turn)
    lane = np.arange(LANES)
    turn = angle(outer[:, None] * lane[None, :], length)
    twiddle = np.stack([np.cos(turn), np.sin(turn)])
    group = lane // half
    k2 = 2 * (lane % half) + group // 2
    imag = group % 2
    turn = angle(lane[:, None] * k2[None, :], LANES)
    cos, sin = np.cos(turn), np.sin(turn)
    top = np.where(imag[None] == 1, -sin, cos)
    bottom = np.where(imag[None] == 1, cos, sin)
    top_swap = np.where(imag[None] == 0, -sin, cos)
    bottom_swap = np.where(imag[None] == 0, cos, sin)
    second = np.concatenate(
        [np.concatenate([top, top_swap], 1), np.concatenate([bottom, bottom_swap], 1)], 0
    )
    turn = angle(k2[:, None] * lane[None, :], LANES)
    cos, sin = np.cos(turn), np.sin(turn)
    third = np.concatenate(
        [np.where(imag[:, None] == 1, -sin, cos), np.where(imag[:, None] == 1, cos, sin)], 1
    )
    turn = angle(np.arange(half)[:, None] * outer[None, :], blocks)
    last = np.concatenate([np.cos(turn), -np.sin(turn)], 1)
    weight = np.full((blocks, LANES), 2.0 / length)
    weight[0, (lane % half == 0) & (group // 2 == 0)] = 1.0 / length
    return [np.asarray(t, np.float32) for t in (first, twiddle, second, third, last, weight)]


def dot(a, b, contract=(1, 0)):
    return lax.dot_general(
        a,
        b,
        (((contract[0],), (contract[1],)), ((), ())),
        precision=HIGHEST,
        preferred_element_type=jnp.float32,
    )


def peer_of(me, d, owners):
    if owners & (owners - 1):
        return lax.rem(me + d, owners)
    bit = 1
    peer = me
    while bit < owners:
        if d & bit:
            peer = peer + bit * (1 - 2 * lax.rem(lax.div(me, bit), 2))
        bit *= 2
    return peer


def kernel(
    dims,
    counts_hbm,
    moment_hbm,
    rupture_hbm,
    source_hbm,
    owner_hbm,
    slab_hbm,
    sgt_hbm,
    slip_hbm,
    first_hbm,
    twiddle_hbm,
    second_hbm,
    third_hbm,
    last_hbm,
    weight_hbm,
    out_ref,
    counts_ref,
    moment_ref,
    rupture_ref,
    source_ref,
    owner_ref,
    slab_ref,
    sgt_ref,
    slip_ref,
    first_ref,
    twiddle_ref,
    second_ref,
    third_ref,
    last_ref,
    weight_ref,
    meta_ref,
    slabs_ref,
    spect_ref,
    acc_ref,
    mine_ref,
    pair_ref,
    sums_ref,
    ring_ref,
    load_sem,
    meta_send,
    meta_recv,
    pair_send,
    pair_recv,
    ring_send,
    ring_recv,
):
    owners, variants, cores, lanes_q, delays, tail_block, tail_rows = dims
    moments, comps, slab_dev, samples = sgt_ref.shape
    ruptures = counts_ref.shape[1]
    rp_dev = moment_ref.shape[1]
    nrp = slab_ref.shape[1]
    functions = slip_ref.shape[0]
    half = samples // LANES
    blocks = 2 * half
    nv = owners * cores
    codes = ceil_to(ruptures, 3) // 3
    me = lax.axis_index("pts")
    my_var = lax.axis_index("var")
    my_core = lax.axis_index("cmp")
    peers = [peer_of(me, d, owners) for d in range(owners)]

    barrier = pltpu.get_barrier_semaphore()
    for d in range(1, owners):
        pl.semaphore_signal(
            barrier, inc=1, device_id={"pts": peers[d]}, device_id_type=MESH
        )
    for c in range(1, cores):
        pl.semaphore_signal(
            barrier, inc=1, device_id={"cmp": lax.rem(my_core + c, cores)}, device_id_type=MESH
        )
    loads = []
    for i, (src, dst) in enumerate(
        (
            (counts_hbm, counts_ref),
            (moment_hbm, moment_ref),
            (owner_hbm, owner_ref),
            (rupture_hbm, rupture_ref),
            (source_hbm, source_ref),
            (slab_hbm, slab_ref),
            (sgt_hbm, sgt_ref),
            (slip_hbm, slip_ref),
            (weight_hbm, weight_ref),
            (first_hbm, first_ref),
            (twiddle_hbm, twiddle_ref),
            (second_hbm, second_ref),
            (third_hbm, third_ref),
            (last_hbm, last_ref),
        )
    ):
        copy = pltpu.make_async_copy(src, dst, load_sem.at[i])
        copy.start()
        loads.append(copy)

    lane = lax.broadcasted_iota(jnp.int32, (1, lanes_q), 1)
    start = me * rp_dev
    slot = lane - start
    inside = (slot >= 0) & (slot < rp_dev)
    zero = jnp.zeros((1, lanes_q), jnp.float32)
    meta_ref[0] = jnp.zeros(meta_ref.shape[1:], jnp.float32)
    slabs_ref[...] = jnp.full(slabs_ref.shape, -1, jnp.int32)
    loads[0].wait()
    loads[1].wait()
    for j in range(moments):
        row = zero
        for l in range(rp_dev):
            row = jnp.where(slot == l, moment_ref[j, l], row)
        meta_ref[0, j : j + 1, :] = row
    total = jnp.int32(0)
    rup_row = jnp.zeros((1, lanes_q), jnp.int32)
    begin_row = jnp.zeros((1, lanes_q), jnp.int32)
    code = [jnp.int32(0)] * codes
    for r in range(ruptures):
        count = counts_ref[0, r]
        total = total + count
        passed = total <= slot
        rup_row = rup_row + passed.astype(jnp.int32)
        begin_row = jnp.where(passed, total, begin_row)
        code[r // 3] = code[r // 3] + count * 256 ** (r % 3)
    for g in range(codes):
        value = code[g].astype(jnp.float32)
        row = moments + 1 + 2 * g
        meta_ref[0, row : row + 1, :] = jnp.where(lane >= start + rp_dev, value, 0.0)
        meta_ref[0, row + 1 : row + 2, :] = zero + value
    meta_ref[0, moments : moments + 1, :] = jnp.where(
        inside, (rup_row + 256 * (slot - begin_row)).astype(jnp.float32), 0.0
    )

    pl.semaphore_wait(barrier, owners + cores - 2)
    order = list(range(owners - 1, 0, -1))
    metas = []
    for d in order:
        copy = pltpu.make_async_remote_copy(
            src_ref=meta_ref.at[0],
            dst_ref=meta_ref.at[d],
            send_sem=meta_send.at[d],
            recv_sem=meta_recv.at[d],
            device_id={"pts": peers[d]},
            device_id_type=MESH,
        )
        copy.start()
        metas.append(copy)

    for copy in loads[2:6]:
        copy.wait()
    slabs_ref[:, :nrp] = slab_ref[...]
    rup_v = jnp.zeros((nv, lanes_q), jnp.float32)
    src_v = jnp.zeros((nv, lanes_q), jnp.float32)
    v_iota = lax.broadcasted_iota(jnp.int32, (nv, lanes_q), 0)
    my_slip = jnp.int32(0)
    for i in range(nv):
        c = lax.rem(my_core + i // owners, cores)
        var_id = owner_ref[(peers[i % owners] * variants + my_var) * cores + c]
        rup_v = jnp.where(v_iota == i, rupture_ref[var_id].astype(jnp.float32), rup_v)
        src_v = jnp.where(v_iota == i, source_ref[0, var_id].astype(jnp.float32), src_v)
        if i == 0:
            my_slip = source_ref[1, var_id]

    loads[6].wait()
    for copy in metas:
        copy.wait()
    merged = meta_ref[0]
    for d in range(1, owners):
        merged = merged + meta_ref[d]
    mixed = merged[moments : moments + 1]
    pos_row = jnp.floor(mixed * (1.0 / 256))
    rup_row = mixed - 256.0 * pos_row
    len_v = jnp.zeros((nv, lanes_q), jnp.float32)
    rest = None
    for r in range(ruptures):
        if r % 3 == 0:
            row = moments + 1 + 2 * (r // 3)
            rest = merged[row : row + 2]
        above = jnp.floor(rest * (1.0 / 256))
        digit = rest - 256.0 * above
        rest = above
        pos_row = pos_row + jnp.where(rup_row == r, digit[0:1], 0.0)
        len_v = len_v + jnp.where(rup_v == r, digit[1:2], 0.0)
    hyp_v = jnp.floor((src_v * len_v + 0.5) * (1.0 / functions))
    apart = jnp.where(rup_v == rup_row, jnp.abs(pos_row - hyp_v), -1.0)
    local = slabs_ref[...] - me * slab_dev
    s_iota = lax.broadcasted_iota(jnp.int32, (slab_dev, lanes_q), 0)
    hit = s_iota == local
    spread = jnp.concatenate(
        [jnp.where(hit, merged[j : j + 1], 0.0) for j in range(moments)] * 2, axis=0
    )
    depth = moments * slab_dev
    upper = lax.broadcasted_iota(jnp.int32, (1, 2 * depth), 1) < depth
    group = delays
    while group * nv > 64 and group % 2 == 0:
        group //= 2
    groups = delays // group
    tail = tail_rows * LANES

    def weights_of(base):
        picks = jnp.concatenate(
            [
                (apart == jnp.float32(delta) + base).astype(jnp.float32)
                for delta in range(group)
            ],
            axis=0,
        )
        weights = dot(picks, spread, (1, 1))
        coarse = weights.astype(jnp.bfloat16).astype(jnp.float32)
        return jnp.where(upper, coarse, weights - coarse).astype(jnp.bfloat16)

    def gathered(pieces, c, begin, acc):
        series = jnp.concatenate([sgt_ref[j, c, :, begin:] for j in range(moments)] * 2, axis=0)
        product = jnp.dot(pieces, series, preferred_element_type=jnp.float32)
        pad = jnp.zeros((nv, tail), jnp.float32)
        for delta in reversed(range(group)):
            term = jnp.concatenate([product[delta * nv : (delta + 1) * nv], pad], axis=1)
            acc = term if acc is None else pltpu.roll(acc, TAU, 1) + term
        return acc

    def offset(c, i, n):
        return i * (tail_block + half) if c == 0 else n * (tail_block + c * half) + i * half

    def rows(c):
        return tail_block + half if c == 0 else half

    def put(c, row, tile):
        for b in range(nv // 8):
            mine_ref[pl.ds(offset(c, b * 8, nv) + row, 8, stride=rows(c)), :] = tile[
                b * 8 : (b + 1) * 8
            ]

    def emit_tail(c, acc, at):
        for e in range(tail_rows):
            put(0, e * comps + c, acc[:, at + e * LANES : at + (e + 1) * LANES])

    def emit(c, acc):
        for t1 in range(half):
            put(c, t1 + (tail_block if c == 0 else 0), acc[:, t1 * LANES : (t1 + 1) * LANES])

    def send_pair(c):
        copies = []
        for k in range(1, cores):
            copy = pltpu.make_async_remote_copy(
                src_ref=mine_ref.at[pl.ds(offset(c, k * owners, nv), owners * rows(c))],
                dst_ref=pair_ref.at[k - 1, pl.ds(offset(c, 0, owners), owners * rows(c))],
                send_sem=pair_send.at[c, k - 1],
                recv_sem=pair_recv.at[c, k - 1],
                device_id={"cmp": lax.rem(my_core + k, cores)},
                device_id_type=MESH,
            )
            copy.start()
            copies.append(copy)
        return copies

    def joined(c, d):
        at = offset(c, d, nv)
        value = mine_ref[at : at + rows(c), :]
        at = offset(c, d, owners)
        for k in range(1, cores):
            value = value + pair_ref[k - 1, at : at + rows(c), :]
        return value

    def place(c):
        return 0 if c == 0 else tail_block + c * half

    def send_ring(c):
        for copy in pairs[c]:
            copy.wait_recv()
        for d in order:
            sums_ref[d - 1, place(c) : place(c) + rows(c), :] = joined(c, d)
        copies = []
        for d in order:
            copy = pltpu.make_async_remote_copy(
                src_ref=sums_ref.at[d - 1, pl.ds(place(c), rows(c))],
                dst_ref=ring_ref.at[d - 1, pl.ds(place(c), rows(c))],
                send_sem=ring_send.at[c, d - 1],
                recv_sem=ring_recv.at[c, d - 1],
                device_id={"pts": peers[d]},
                device_id_type=MESH,
            )
            copy.start()
            copies.append(copy)
        return copies

    for i in range(nv):
        at = offset(0, i, nv)
        mine_ref[at : at + tail_block, :] = jnp.zeros((tail_block, LANES), jnp.float32)
    pairs, rings = [], []
    if groups > 1:
        acc_ref[...] = jnp.zeros(acc_ref.shape, jnp.float32)

        def one_group(step, carry):
            base = lax.convert_element_type((groups - 1 - step) * group, jnp.float32)
            pieces = weights_of(base)
            for c in range(comps):
                acc_ref[c] = gathered(pieces, c, 0, acc_ref[c])
            return carry

        lax.fori_loop(0, groups, one_group, 0)
        for c in range(comps):
            emit_tail(c, acc_ref[c], samples)
        for c in range(comps):
            emit(c, acc_ref[c])
            pairs.append(send_pair(c))
        for c in range(comps):
            rings.append(send_ring(c))
    else:
        pieces = weights_of(0.0)
        for c in range(comps):
            emit_tail(c, gathered(pieces, c, samples - tail, None), tail)
        for c in range(comps):
            emit(c, gathered(pieces, c, 0, None))
            pairs.append(send_pair(c))
            if c > 0:
                rings.append(send_ring(c - 1))
        rings.append(send_ring(comps - 1))

    loads[7].wait()
    for a in range(half):
        real = slip_ref[my_slip, 0:1, a * LANES : (a + 1) * LANES]
        imag = slip_ref[my_slip, 1:2, a * LANES : (a + 1) * LANES]
        spect_ref[a : a + 1, :] = real
        spect_ref[half + a : half + a + 1, :] = real
        spect_ref[2 * half + a : 2 * half + a + 1, :] = -imag
        spect_ref[3 * half + a : 3 * half + a + 1, :] = imag
    turned = jnp.transpose(spect_ref[...])
    for copy in loads[8:]:
        copy.wait()
    slip_real = weight_ref[...] * jnp.concatenate(
        [turned[:blocks, :blocks], turned[blocks:, :blocks]], axis=1
    )
    slip_imag = weight_ref[...] * jnp.concatenate(
        [turned[:blocks, blocks:], turned[blocks:, blocks:]], axis=1
    )
    cos, sin = twiddle_ref[0], twiddle_ref[1]
    tails = None
    for c in range(comps):
        packed = joined(c, 0)
        for copy in rings[c]:
            copy.wait_recv()
        for d in range(1, owners):
            packed = packed + ring_ref[d - 1, place(c) : place(c) + rows(c), :]
        if c == 0:
            tails = packed[:tail_block]
        else:
            packed = jnp.concatenate([tails, packed], axis=0)
        stage = dot(first_ref[c], packed)
        real, imag = stage[:blocks], stage[blocks:]
        turn = jnp.concatenate([real * cos + imag * sin, imag * cos - real * sin], axis=1)
        spectra = dot(turn, second_ref[...])
        spectra = spectra[:, :LANES] * slip_real + spectra[:, LANES:] * slip_imag
        middle = dot(spectra, third_ref[...])
        real, imag = middle[:, :LANES], middle[:, LANES:]
        turn = jnp.concatenate([real * cos - imag * sin, real * sin + imag * cos], axis=0)
        out_ref[c] = dot(last_ref[...], turn)
    for copies in pairs + rings:
        for copy in copies:
            copy.wait_send()


def per_device(owners, variants, cores, *args):
    sgt, moment, slip_spec, rp_slab, rup_counts, var_rupture, var_source, owner_map = args
    moments, comps, slab_dev, samples = sgt.shape
    nrp = rp_slab.shape[0]
    half = samples // LANES
    nv = owners * cores
    assert owner_map.shape[0] == nv * variants and 4 * half == LANES and nv % 8 == 0
    assert MOST * owners < 256 and moments + 1 + 2 * (ceil_to(rup_counts.shape[1], 3) // 3) <= 8
    lanes_q = ceil_to(nrp, LANES)
    delays = MOST * owners
    tail_rows = ceil_to(TAU * (delays - 1), LANES) // LANES
    width = samples + tail_rows * LANES
    tail_block = ceil_to(comps * tail_rows, 8)
    pitch = tail_block + comps * half
    consts = tables(comps, samples, tail_rows, tail_block)
    dims = (owners, variants, cores, lanes_q, delays, tail_block, tail_rows)
    f32 = jnp.float32
    others = max(owners - 1, 1)
    vmem = pl.BlockSpec(memory_space=pltpu.VMEM)
    anywhere = pl.BlockSpec(memory_space=pl.ANY)
    out = pl.pallas_call(
        functools.partial(kernel, dims),
        out_shape=jax.ShapeDtypeStruct((comps, half, LANES), f32),
        in_specs=[anywhere] * 14,
        out_specs=vmem,
        scratch_shapes=[
            pltpu.SMEM(rup_counts.shape, jnp.int32),
            pltpu.SMEM(moment.shape, f32),
            pltpu.SMEM(var_rupture.shape, jnp.int32),
            pltpu.SMEM(var_source.shape[::-1], jnp.int32),
            pltpu.SMEM(owner_map.shape, jnp.int32),
            pltpu.VMEM((1, nrp), jnp.int32),
            pltpu.VMEM(sgt.shape, sgt.dtype),
            pltpu.VMEM(slip_spec.shape, f32),
            *[pltpu.VMEM(t.shape, f32) for t in consts],
            pltpu.VMEM((owners, 8, lanes_q), f32),
            pltpu.VMEM((1, lanes_q), jnp.int32),
            pltpu.VMEM((LANES, LANES), f32),
            pltpu.VMEM((comps, nv, width) if nv * delays > 64 else (1, 8, LANES), f32),
            pltpu.VMEM((nv * pitch, LANES), f32),
            pltpu.VMEM((cores - 1, owners * pitch, LANES), f32),
            pltpu.VMEM((others, pitch, LANES), f32),
            pltpu.VMEM((others, pitch, LANES), f32),
            pltpu.SemaphoreType.DMA((14,)),
            pltpu.SemaphoreType.DMA((owners,)),
            pltpu.SemaphoreType.DMA((owners,)),
            pltpu.SemaphoreType.DMA((comps, cores)),
            pltpu.SemaphoreType.DMA((comps, cores)),
            pltpu.SemaphoreType.DMA((comps, owners)),
            pltpu.SemaphoreType.DMA((comps, owners)),
        ],
        compiler_params=pltpu.CompilerParams(collective_id=0, has_side_effects=True),
    )(
        rup_counts,
        moment,
        var_rupture,
        var_source.T,
        owner_map,
        rp_slab.reshape(1, nrp),
        sgt,
        slip_spec,
        *[jnp.asarray(t) for t in consts],
    )
    return out.reshape(1, comps, samples)


def solution(mesh):
    placed = (
        P("cmp", None, ("site", "pts"), None),
        P("cmp", ("site", "pts")),
        P(),
        P("site"),
        P(("site", "pts"), None),
        P("site"),
        P("site", None),
        P("site"),
    )
    sizes = (mesh.shape["pts"], mesh.shape["var"], mesh.shape["cmp"])
    return jax.shard_map(
        functools.partial(per_device, *sizes),
        mesh=mesh,
        in_specs=placed,
        out_specs=P(("site", "pts", "var", "cmp"), None, None),
        check_vma=False,
    )
```

time: 22.4 us -> 21.2 us (0.946)
  the two profiles are of different devices: /device:TPU:1 before, /device:TPU:0 now
where the time goes in v2:
time: 21.2 us; the launch traced here: 21 us
  Pallas kernels  19.6 us (92%)
  local copies, waits for them, and re-layouts  1.42 us (7%)
    pallas_call x1, Pallas kernels, per_device(): pl.pallas_call(functools.partial(kernel, dims), out_shape=jax.ShapeDtypeS...  19.6 us
    unnamed x1, local copies, waits for them, and re-layouts  1.42 us

profile of v2, /device:TPU:0, one launch (start us, length us, event | category | flops | bytes accessed | tf_op | source)
XLA Modules:
  0.0 21.0 jit_solution(8677877730172879796)
XLA Ops:
  0.0 19.6 %shard_map.136 = f32[3,32,128]{2,1,0:T(8,128)} custom-call(s32[1,6]{1,0:T(1,128)} %counts_hbm.1, f32[3,8]{1,0:T(4,128)} %moment_hbm.1, s32[16]{0:T(128)} %rupture_hbm.1, s32[2,16]{1,0:T(2,128)} %bitcast.4, s32[16]{0:T(128)} %owner_hbm.1, s32[1,32]{1,0:T(1,128)} %bitcast.5, bf16[3,3,16,4096]{3,2,1,0:T(8,128)(2,1)} %sgt_hbm.1, f32[16,2,4096]{2,1,0:T(2,128)} %slip_hbm.1, ...), custom_call_target="tpu_custom_call" | custom-call | tf_op jit(solution)/shard_map/pallas_call | solution.py:464
  19.6 1.4 %copy.18 = f32[1,3,4096]{2,0,1:T(1,128)} copy(f32[1,3,4096]{2,0,1:T(1,128)} %bitcast.3) | data formatting | bytes 98304

commit v3 on v2

--- a/solution.py
+++ b/solution.py
@@ -60,7 +60,19 @@
     last = np.concatenate([np.cos(turn), -np.sin(turn)], 1)
     weight = np.full((blocks, LANES), 2.0 / length)
     weight[0, (lane % half == 0) & (group // 2 == 0)] = 1.0 / length
-    return [np.asarray(t, np.float32) for t in (first, twiddle, second, third, last, weight)]
+
+    def pieces(table, axis=0):
+        coarse = table.astype(jnp.bfloat16)
+        return np.stack([coarse, (table - coarse.astype(np.float64)).astype(jnp.bfloat16)], axis)
+
+    return [
+        pieces(first, 1),
+        twiddle.astype(np.float32),
+        pieces(second),
+        pieces(third),
+        pieces(last),
+        weight.astype(np.float32),
+    ]
 
 
 def dot(a, b, contract=(1, 0)):
@@ -70,6 +82,31 @@
         (((contract[0],), (contract[1],)), ((), ())),
         precision=HIGHEST,
         preferred_element_type=jnp.float32,
+    )
+
+
+def halves(value):
+    coarse = value.astype(jnp.bfloat16)
+    return coarse, (value - coarse.astype(jnp.float32)).astype(jnp.bfloat16)
+
+
+def right(a, table):
+    coarse, fine = halves(a)
+    big, small = table[0], table[1]
+    return (
+        jnp.dot(coarse, small, preferred_element_type=jnp.float32)
+        + jnp.dot(fine, big, preferred_element_type=jnp.float32)
+        + jnp.dot(coarse, big, preferred_element_type=jnp.float32)
+    )
+
+
+def left(table, b):
+    coarse, fine = halves(b)
+    big, small = table[0], table[1]
+    return (
+        jnp.dot(small, coarse, preferred_element_type=jnp.float32)
+        + jnp.dot(big, fine, preferred_element_type=jnp.float32)
+        + jnp.dot(big, coarse, preferred_element_type=jnp.float32)
     )
 
 
@@ -394,9 +431,8 @@
         for c in range(comps):
             emit(c, gathered(pieces, c, 0, None))
             pairs.append(send_pair(c))
-            if c > 0:
-                rings.append(send_ring(c - 1))
-        rings.append(send_ring(comps - 1))
+        for c in range(comps):
+            rings.append(send_ring(c))
 
     loads[7].wait()
     for a in range(half):
@@ -427,15 +463,15 @@
             tails = packed[:tail_block]
         else:
             packed = jnp.concatenate([tails, packed], axis=0)
-        stage = dot(first_ref[c], packed)
+        stage = left(first_ref.at[c], packed)
         real, imag = stage[:blocks], stage[blocks:]
         turn = jnp.concatenate([real * cos + imag * sin, imag * cos - real * sin], axis=1)
-        spectra = dot(turn, second_ref[...])
+        spectra = right(turn, second_ref)
         spectra = spectra[:, :LANES] * slip_real + spectra[:, LANES:] * slip_imag
-        middle = dot(spectra, third_ref[...])
+        middle = right(spectra, third_ref)
         real, imag = middle[:, :LANES], middle[:, LANES:]
         turn = jnp.concatenate([real * cos - imag * sin, real * sin + imag * cos], axis=0)
-        out_ref[c] = dot(last_ref[...], turn)
+        out_ref[c] = left(last_ref, turn)
     for copies in pairs + rings:
         for copy in copies:
             copy.wait_send()
@@ -463,7 +499,7 @@
     anywhere = pl.BlockSpec(memory_space=pl.ANY)
     out = pl.pallas_call(
         functools.partial(kernel, dims),
-        out_shape=jax.ShapeDtypeStruct((comps, half, LANES), f32),
+        out_shape=pltpu.VMEM((comps, half, LANES), f32),
         in_specs=[anywhere] * 14,
         out_specs=vmem,
         scratch_shapes=[
@@ -475,7 +511,7 @@
             pltpu.VMEM((1, nrp), jnp.int32),
             pltpu.VMEM(sgt.shape, sgt.dtype),
             pltpu.VMEM(slip_spec.shape, f32),
-            *[pltpu.VMEM(t.shape, f32) for t in consts],
+            *[pltpu.VMEM(t.shape, t.dtype) for t in consts],
             pltpu.VMEM((owners, 8, lanes_q), f32),
             pltpu.VMEM((1, lanes_q), jnp.int32),
             pltpu.VMEM((LANES, LANES), f32),

time: 21.2 us -> 20.2 us (0.953)
  local copies, waits for them, and re-layouts: 1.42 us -> 0.62 us
    unnamed x1, local copies, waits for them, and re-layouts: 1.42 us -> 0.62 us
where the time goes in v3:
time: 20.2 us; the launch traced here: 20.1 us
  Pallas kernels  19.4 us (96%)
  local copies, waits for them, and re-layouts  0.62 us (3%)
    pallas_call x1, Pallas kernels, per_device(): pl.pallas_call(functools.partial(kernel, dims), out_shape=pltpu.VMEM((com...  19.4 us
    unnamed x1, local copies, waits for them, and re-layouts  0.62 us

profile of v3, /device:TPU:0, one launch (start us, length us, event | category | flops | bytes accessed | tf_op | source)
XLA Modules:
  0.0 20.1 jit_solution(1062232625170390309)
XLA Ops:
  0.0 19.4 %shard_map.136 = f32[3,32,128]{2,1,0:T(8,128)S(1)} custom-call(s32[1,6]{1,0:T(1,128)} %counts_hbm.1, f32[3,8]{1,0:T(4,128)} %moment_hbm.1, s32[16]{0:T(128)} %rupture_hbm.1, s32[2,16]{1,0:T(2,128)} %bitcast.4, s32[16]{0:T(128)} %owner_hbm.1, s32[1,32]{1,0:T(1,128)} %bitcast.5, bf16[3,3,16,4096]{3,2,1,0:T(8,128)(2,1)} %sgt_hbm.1, f32[16,2,4096]{2,1,0:T(2,128)} %slip_hbm.1, ...), custom_call_target="tpu_custom_call" | custom-call | tf_op jit(solution)/shard_map/pallas_call | solution.py:500
  19.5 0.6 %copy.18 = f32[1,3,4096]{2,0,1:T(1,128)} copy(f32[1,3,4096]{2,0,1:T(1,128)S(1)} %bitcast.3) | data formatting | bytes 98304

commit v4 on v1

--- a/solution.py
+++ b/solution.py
@@ -61,7 +61,18 @@
     last = np.concatenate([np.cos(turn), -np.sin(turn)], 1)
     weight = np.full((blocks, LANES), 2.0 / length)
     weight[0, (lane % half == 0) & (group // 2 == 0)] = 1.0 / length
-    return [np.asarray(t, np.float32) for t in (first, twiddle, second, third, last, weight)]
+    def pieces(table, axis=0):
+        coarse = table.astype(jnp.bfloat16)
+        return np.stack([coarse, (table - coarse.astype(np.float64)).astype(jnp.bfloat16)], axis)
+
+    return [
+        pieces(first),
+        twiddle.astype(np.float32),
+        pieces(second),
+        pieces(third),
+        pieces(last),
+        weight.astype(np.float32),
+    ]
 
 
 def dot(a, b, contract=(1, 0)):
@@ -71,6 +82,31 @@
         (((contract[0],), (contract[1],)), ((), ())),
         precision=HIGHEST,
         preferred_element_type=jnp.float32,
+    )
+
+
+def halves(value):
+    coarse = value.astype(jnp.bfloat16)
+    return coarse, (value - coarse.astype(jnp.float32)).astype(jnp.bfloat16)
+
+
+def right(a, table):
+    coarse, fine = halves(a)
+    big, small = table[0], table[1]
+    return (
+        jnp.dot(coarse, small, preferred_element_type=jnp.float32)
+        + jnp.dot(fine, big, preferred_element_type=jnp.float32)
+        + jnp.dot(coarse, big, preferred_element_type=jnp.float32)
+    )
+
+
+def left(table, b):
+    coarse, fine = halves(b)
+    big, small = table[0], table[1]
+    return (
+        jnp.dot(small, coarse, preferred_element_type=jnp.float32)
+        + jnp.dot(big, fine, preferred_element_type=jnp.float32)
+        + jnp.dot(big, coarse, preferred_element_type=jnp.float32)
     )
 
 
@@ -140,8 +176,8 @@
     loads = []
     for i, (src, dst) in enumerate(
         (
+            (sgt_hbm, sgt_ref),
             (slip_hbm, slip_ref),
-            (sgt_hbm, sgt_ref),
             (weight_hbm, weight_ref),
             (first_hbm, first_ref),
             (twiddle_hbm, twiddle_ref),
@@ -193,9 +229,9 @@
         c = lax.rem(my_core + i // owners, cores)
         var_id = owner_ref[(p * variants + my_var) * cores + c]
         rup_v = jnp.where(v_iota == i, rupture_ref[var_id].astype(jnp.float32), rup_v)
-        src_v = jnp.where(v_iota == i, source_ref[var_id, 0].astype(jnp.float32), src_v)
+        src_v = jnp.where(v_iota == i, source_ref[0, var_id].astype(jnp.float32), src_v)
         if i == 0:
-            my_slip = source_ref[var_id, 1]
+            my_slip = source_ref[1, var_id]
 
     pl.semaphore_wait(barrier, owners + cores - 2)
     metas = []
@@ -212,25 +248,6 @@
         metas.append(copy)
 
     loads[0].wait()
-    for a in range(half):
-        real = slip_ref[my_slip, 0:1, a * LANES : (a + 1) * LANES]
-        imag = slip_ref[my_slip, 1:2, a * LANES : (a + 1) * LANES]
-        spect_ref[a : a + 1, :] = real
-        spect_ref[half + a : half + a + 1, :] = real
-        spect_ref[2 * half + a : 2 * half + a + 1, :] = -imag
-        spect_ref[3 * half + a : 3 * half + a + 1, :] = imag
-    turned = jnp.transpose(spect_ref[...])
-    loads[2].wait()
-    slip_real = weight_ref[...] * jnp.concatenate(
-        [turned[:blocks, :blocks], turned[blocks:, :blocks]], axis=1
-    )
-    slip_imag = weight_ref[...] * jnp.concatenate(
-        [turned[:blocks, blocks:], turned[blocks:, blocks:]], axis=1
-    )
-    spect_ref[:blocks, :] = slip_real
-    spect_ref[blocks:, :] = slip_imag
-
-    loads[1].wait()
     for copy in metas:
         copy.wait()
     merged = meta_ref[0]
@@ -325,8 +342,6 @@
         )
         copy.start()
         pairs.append(copy)
-    for copy in loads[3:]:
-        copy.wait()
     for copy in pairs:
         copy.wait_recv()
     order = sorted(range(1, owners), key=lambda d: -min(d, owners - d))
@@ -351,13 +366,33 @@
         )
         copy.start()
         rings.append(copy)
+    loads[1].wait()
+    for a in range(half):
+        real = slip_ref[my_slip, 0:1, a * LANES : (a + 1) * LANES]
+        imag = slip_ref[my_slip, 1:2, a * LANES : (a + 1) * LANES]
+        spect_ref[a : a + 1, :] = real
+        spect_ref[half + a : half + a + 1, :] = real
+        spect_ref[2 * half + a : 2 * half + a + 1, :] = -imag
+        spect_ref[3 * half + a : 3 * half + a + 1, :] = imag
+    turned = jnp.transpose(spect_ref[...])
+    for copy in loads[2:]:
+        copy.wait()
+    slip_real = weight_ref[...] * jnp.concatenate(
+        [turned[:blocks, :blocks], turned[blocks:, :blocks]], axis=1
+    )
+    slip_imag = weight_ref[...] * jnp.concatenate(
+        [turned[:blocks, blocks:], turned[blocks:, blocks:]], axis=1
+    )
+    spect_ref[:blocks, :] = slip_real
+    spect_ref[blocks:, :] = slip_imag
+
     packed = joined(0)
     for copy in rings:
         copy.wait_recv()
     for d in range(1, owners):
         packed = packed + ring_ref[d - 1]
 
-    stage = dot(first_ref[...], packed)
+    stage = left(first_ref, packed)
     cos, sin = twiddle_ref[0], twiddle_ref[1]
     rows = []
     for c in range(comps):
@@ -366,13 +401,13 @@
         rows.append(
             jnp.concatenate([real * cos + imag * sin, imag * cos - real * sin], axis=1)
         )
-    spectra = dot(jnp.concatenate(rows, axis=0), second_ref[...])
+    spectra = right(jnp.concatenate(rows, axis=0), second_ref)
     slip_real, slip_imag = spect_ref[:blocks, :], spect_ref[blocks:, :]
     rows = []
     for c in range(comps):
         part = spectra[c * blocks : (c + 1) * blocks]
         rows.append(part[:, :LANES] * slip_real + part[:, LANES:] * slip_imag)
-    middle = dot(jnp.concatenate(rows, axis=0), third_ref[...])
+    middle = right(jnp.concatenate(rows, axis=0), third_ref)
     columns = []
     for c in range(comps):
         real = middle[c * blocks : (c + 1) * blocks, :LANES]
@@ -380,7 +415,7 @@
         columns.append(
             jnp.concatenate([real * cos - imag * sin, real * sin + imag * cos], axis=0)
         )
-    result = dot(last_ref[...], jnp.concatenate(columns, axis=1))
+    result = left(last_ref, jnp.concatenate(columns, axis=1))
     for c in range(comps):
         out_ref[c] = result[:, c * LANES : (c + 1) * LANES]
     for copy in pairs + rings:
@@ -409,13 +444,13 @@
     anywhere = pl.BlockSpec(memory_space=pl.ANY)
     out = pl.pallas_call(
         functools.partial(kernel, dims),
-        out_shape=jax.ShapeDtypeStruct((comps, half, LANES), f32),
+        out_shape=pltpu.VMEM((comps, half, LANES), f32),
         in_specs=[smem] * 5 + [vmem] + [anywhere] * 8,
         out_specs=vmem,
         scratch_shapes=[
             pltpu.VMEM(sgt.shape, sgt.dtype),
             pltpu.VMEM(slip_spec.shape, f32),
-            *[pltpu.VMEM(t.shape, f32) for t in consts],
+            *[pltpu.VMEM(t.shape, t.dtype) for t in consts],
             pltpu.VMEM((owners, 24, lanes_q), f32),
             pltpu.VMEM((1, lanes_q), jnp.int32),
             pltpu.VMEM((LANES, LANES), f32),
@@ -437,7 +472,7 @@
         rup_counts,
         moment,
         var_rupture,
-        var_source,
+        var_source.T,
         owner_map,
         rp_slab.reshape(1, nrp),
         sgt,

time: 22.4 us -> 18.9 us (0.84)
  local copies, waits for them, and re-layouts: 2.77 us -> 0.62 us
  Pallas kernels: 19.4 us -> 18.1 us
    unnamed x2 -> x1, local copies, waits for them, and re-layouts: 2.77 us -> 0.62 us
    pallas_call x1, Pallas kernels: 19.4 us -> 18.1 us  [per_device(): pl.pallas_call(functools.partial(kernel, dims), out_shape=pltpu.VMEM((com...]
where the time goes in v4:
time: 18.9 us; the launch traced here: 18.8 us
  Pallas kernels  18.1 us (96%)
  local copies, waits for them, and re-layouts  0.62 us (3%)
    pallas_call x1, Pallas kernels, per_device(): pl.pallas_call(functools.partial(kernel, dims), out_shape=pltpu.VMEM((com...  18.1 us
    unnamed x1, local copies, waits for them, and re-layouts  0.62 us

profile of v4, /device:TPU:1, one launch (start us, length us, event | category | flops | bytes accessed | tf_op | source)
XLA Modules:
  0.0 18.8 jit_solution(16679698011131904825)
XLA Ops:
  0.0 18.1 %shard_map.136 = f32[3,32,128]{2,1,0:T(8,128)S(1)} custom-call(s32[1,6]{1,0:T(1,128)} %counts_ref.1, f32[3,8]{1,0:T(4,128)} %moment_ref.1, s32[16]{0:T(128)} %rupture_ref.1, s32[2,16]{1,0:T(2,128)} %bitcast.4, s32[16]{0:T(128)} %owner_ref.1, s32[1,32]{1,0:T(1,128)} %bitcast.5, bf16[3,3,16,4096]{3,2,1,0:T(8,128)(2,1)} %sgt_hbm.1, f32[16,2,4096]{2,1,0:T(2,128)} %slip_hbm.1, ...), custom_call_target="tpu_custom_call" | custom-call | tf_op jit(solution)/shard_map/pallas_call | solution.py:445
  18.1 0.6 %copy.18 = f32[1,3,4096]{2,0,1:T(1,128)} copy(f32[1,3,4096]{2,0,1:T(1,128)S(1)} %bitcast.3) | data formatting | bytes 98304
